TPU v7x, 256 devices: a whole 4x4x8 slice. The times are simulated.
256 devices in a mesh: tok: 128 (over x, z, y), exp: 2 (over core).
Axes of the slice: x: 4, y: 4, z: 8, core: 2. Of those that a mesh axis runs over, the one named last changes fastest.
Arguments:
- activations: bfloat16 [3072, 14336], P(('tok', 'exp')), may hold values from -6 to 6
- expert_ids: int32 [3072, 2], P(('tok', 'exp')), may hold values from 0 to 7, all different within a row; in each aligned block of 12 rows (0 to 11, 12 to 23, ...) at most 4 rows name the same one
Outputs:
- hessian: float32 [2, 14336, 14336], P('exp', 'tok')
Inputs may be any that keep to these rules, and one draw needn't show every extreme that they name: `expert_ids`: each row names 2 different experts. Among the 12 rows of one device no expert is named more than 4 times, some expert exactly 4 times; every expert is named by some row.
All inputs are finite; a program needn't handle non-finite values.
Results may differ from a plain program's by a relative error of at most 0.0003.
Values may be sent and summed in bfloat16 or wider, within the bound.
A program may use at most 128 MiB of HBM per device.

v0:
```python
import jax
import jax.numpy as jnp
from jax import lax
from jax.sharding import Mesh
from jax.sharding import PartitionSpec as P

CAP = 4
LANES = 128
RING = "tok_2"
PLANE = ("tok_0", "tok_1")
TOK = ("tok_0", "tok_1", "tok_2")
TOK_EXP = ("tok_0", "tok_1", "tok_2", "exp")


def place_tokens(activations, expert_ids, window_size):
    expert_labels = jnp.arange(window_size, dtype=jnp.int32)
    routed = jnp.any(expert_ids[:, :, None] == expert_labels[None, None, :], axis=1).astype(
        jnp.int32
    )
    ranking = jnp.cumsum(routed, axis=0) - 1
    slot_labels = jnp.arange(CAP, dtype=jnp.int32)
    placement = (routed.T[:, None, :] == 1) & (ranking.T[:, None, :] == slot_labels[None, :, None])
    placement_b = placement.astype(jnp.bfloat16)
    send_slots = jnp.einsum(
        "gct,tf->gcf", placement_b, activations, preferred_element_type=jnp.float32
    ).astype(jnp.bfloat16)
    return (send_slots, jnp.sum(routed, axis=0))


def shards(activations, expert_ids):
    experts = lax.axis_size("exp")
    ring = lax.axis_size(RING)
    ff = activations.shape[1]
    tiles = ff // (ring * LANES)
    slots, counts = place_tokens(activations, expert_ids, experts)
    slots = slots.reshape(experts, CAP, tiles, ring, LANES).transpose(3, 0, 1, 2, 4)
    slots = slots.reshape(ring * experts, CAP, tiles * LANES)
    own = lax.all_to_all(slots, (RING, "exp"), split_axis=0, concat_axis=0, tiled=True)
    own = own.reshape(ring * experts * CAP, tiles * LANES)
    total = counts.astype(jnp.float32)
    for axis in TOK_EXP:
        total = lax.psum(total, axis)
    routed_total = total[lax.axis_index("exp")]
    cols = lax.all_gather(own, PLANE, axis=0, tiled=True)
    group = lax.axis_index("tok_0") * lax.axis_size("tok_1") + lax.axis_index("tok_1")
    rows = ff // lax.axis_size(PLANE)
    first = group * rows // LANES
    y = lax.axis_index(RING)
    mine = (first - y + ring - 1) // ring
    left = lax.dynamic_slice_in_dim(cols, mine * LANES, LANES, axis=1)
    left = lax.all_gather(left, RING, axis=0)
    order = (first + jnp.arange(ring)) % ring
    left = jnp.take(left, order, axis=0).transpose(1, 0, 2).reshape(cols.shape[0], ring * LANES)
    left = lax.dynamic_slice_in_dim(left, group * rows - first * LANES, rows, axis=1)
    product = lax.dot_general(
        left, cols, (((0,), (0,)), ((), ())), preferred_element_type=jnp.float32
    )
    out = lax.all_to_all(
        product.reshape(ring, rows // ring, tiles * LANES),
        RING,
        split_axis=0,
        concat_axis=0,
        tiled=True,
    )
    out = out * (2.0 / routed_total)
    out = out.reshape(ring, rows // ring, tiles, LANES).transpose(1, 2, 0, 3)
    return out.reshape(1, rows // ring, ff)


def solution(mesh):
    split = Mesh(
        mesh.devices.reshape(4, 8, 4, mesh.shape["exp"]), ("tok_0", "tok_1", "tok_2", "exp")
    )
    return jax.shard_map(
        shards,
        mesh=split,
        in_specs=(P(TOK_EXP, None), P(TOK_EXP, None)),
        out_specs=P("exp", TOK, None),
        check_vma=False,
    )
```

profile of v0, /device:TPU:1, one launch (start us, length us, event | category | flops | bytes accessed | tf_op | source)
XLA Modules:
  0.0 275.6 jit_solution(9909398859649748255)
XLA Ops:
  6.5 0.0 copy-start
  6.5 0.7 compare_reduce_fusion
  7.3 0.2 reduce_window_sum.11
  7.5 0.1 copy-done
  7.6 0.2 convolution_convert_fusion
  7.8 0.1 reshape.81
  8.0 0.1 reshape.82
  8.1 0.1 copy.18
  8.3 11.9 %all_to_all.10 = bf16[8,4,3584]{2,1,0:T(4,128)(2,1)S(1)} all-to-all(bf16[8,4,3584]{2,1,0:T(4,128)(2,1)S(1)} %copy.18), channel_id=1, replica_groups=mesh['tok_0'=4,'tok_1'=8,'tok_2'=4,'exp'=2] {'tok_2','exp'}, dimensions={0} | all-to-all | bytes 458752 | tf_op jit(solution)/shard_map/all_to_all | solution.py:38
  20.2 0.7 reshape.83
  20.9 0.0 all-gather.4.cloned.1.call-update
  21.0 0.0 all-gather.6.cloned.1.call-start
  21.1 93.6 %all-gather.4.cloned.1.call-done = bf16[1024,3584]{1,0:T(8,128)(2,1)} async-done(((bf16[32,3584]{1,0:T(8,128)(2,1)}), bf16[1024,3584]{1,0:T(8,128)(2,1)}) %all-gather.4.cloned.1.call-update) | async-done | bytes 7340048 | tf_op jit(solution)/shard_map/all_gather | solution.py:44
  114.7 1.7 constant_dynamic-slice_fusion
  116.3 0.0 all-gather.6.cloned.1.call-update
  116.4 22.4 %all-gather.6.cloned.1.call-done = bf16[4096,128]{1,0:T(8,128)(2,1)} async-done(((bf16[1024,128]{1,0:T(8,128)(2,1)}), bf16[4096,128]{1,0:T(8,128)(2,1)}) %all-gather.6.cloned.1.call-update) | async-done | bytes 1048592 | tf_op jit(solution)/shard_map/all_gather | solution.py:51
  138.8 2.0 gather_fusion
  140.8 0.2 select_bitcast_fusion
  141.0 0.5 copy.19
  141.5 8.5 %fusion = f32[448,3584]{1,0:T(8,128)} fusion(bf16[1024,3584]{1,0:T(8,128)(2,1)} %all-gather.4.cloned.1.call-done, bf16[1024,512]{0,1:T(8,128)(2,1)S(1)} %bitcast.25, s32[]{:T(128)S(6)} %select_n.67), kind=kOutput, calls=%fused_computation.4 | convolution fusion | flops 3288334336 | bytes 14680068 | tf_op jit(solution)/shard_map/dot_general | solution.py:55
  150.0 5.3 %all-to-all-start.1 = ((f32[4,112,3584]{2,1,0:T(8,128)}), f32[4,112,3584]{2,1,0:T(8,128)}, u32[]{:S(2)}, u32[]{:S(2)}) async-start(f32[4,112,3584]{2,1,0:T(8,128)} %bitcast.23), calls=%async_computation.1 | async-start | bytes 12845056 | tf_op jit(solution)/shard_map/all_to_all | solution.py:58
  155.3 0.1 convert_reduce_fusion
  155.4 8.8 %psum.28 = f32[2]{0:T(128)S(1)} all-reduce(f32[2]{0:T(128)S(1)} %convert_element_type.14), channel_id=1, replica_groups=mesh['tok_0'=4,'tok_1'=8,'tok_2'=4,'exp'=2] {'tok_0'}, use_global_device_ids=true, to_apply=%region_3.4 | all-reduce | flops 2 | bytes 16 | tf_op jit(solution)/shard_map/psum | solution.py:42
  164.2 15.3 %psum.29 = f32[2]{0:T(128)S(1)} all-reduce(f32[2]{0:T(128)S(1)} %psum.28), channel_id=1, replica_groups=mesh['tok_0'=4,'tok_1'=8,'tok_2'=4,'exp'=2] {'tok_1'}, use_global_device_ids=true, to_apply=%region_4.5 | all-reduce | flops 2 | bytes 16 | tf_op jit(solution)/shard_map/psum | solution.py:42
  179.5 48.1 %psum.30 = f32[2]{0:T(128)S(1)} all-reduce(f32[2]{0:T(128)S(1)} %psum.29), channel_id=1, replica_groups=mesh['tok_0'=4,'tok_1'=8,'tok_2'=4,'exp'=2] {'tok_2'}, use_global_device_ids=true, to_apply=%region_5.6 | all-reduce | flops 2 | bytes 16 | tf_op jit(solution)/shard_map/psum | solution.py:42
  227.5 5.9 %psum.31 = f32[2]{0:T(128)S(1)} all-reduce(f32[2]{0:T(128)S(1)} %psum.30), channel_id=1, replica_groups=mesh['tok_0'=4,'tok_1'=8,'tok_2'=4,'exp'=2] {'exp'}, use_global_device_ids=true, to_apply=%region_6.7 | all-reduce | flops 2 | bytes 16 | tf_op jit(solution)/shard_map/psum | solution.py:42
  233.4 0.6 dynamic_slice.11
  234.6 0.0 all-to-all-done.1
  234.6 6.0 %broadcast_multiply_fusion = f32[4,112,3584]{2,1,0:T(8,128)} fusion(f32[4,112,3584]{2,1,0:T(8,128)} %all-to-all-done.1, f32[]{:T(128)} %bitcast.9), kind=kLoop, calls=%fused_computation.2 | loop fusion | flops 1605632 | bytes 12845060 | tf_op jit(solution)/shard_map/mul | solution.py:65
  240.6 7.9 %reshape.86 = f32[4,112,28,128]{3,2,1,0:T(8,128)} reshape(f32[4,112,3584]{2,1,0:T(8,128)} %broadcast_multiply_fusion) | data formatting | bytes 12845056 | tf_op jit(solution)/shard_map/reshape | solution.py:66
  248.5 12.1 %copy.20 = f32[112,28,4,128]{3,2,1,0:T(4,128)} copy(f32[112,28,4,128]{3,1,0,2:T(8,128)} %bitcast.22) | data formatting | bytes 12845056 | tf_op jit(solution)/shard_map/transpose | solution.py:66
  260.6 8.2 %reshape.87 = f32[1,112,14336]{2,1,0:T(8,128)} reshape(f32[112,28,4,128]{3,2,1,0:T(4,128)} %copy.20) | data formatting | bytes 12845056 | tf_op jit(solution)/shard_map/reshape | solution.py:67
  (8 shorter events, 0.1 us)
Async XLA Ops:
  6.5 1.0 copy-start
  6.5 108.1 %all-gather.4.cloned.1.call-start = ((), (), s32[]{:S(2)}) async-start(), calls=%async_computation.2 | async-start | bytes 7569408 | tf_op jit(solution)/shard_map/all_gather | solution.py:44
  21.0 117.9 %all-gather.6.cloned.1.call-start = ((), (), s32[]{:S(2)}) async-start(), calls=%async_computation.3 | async-start | bytes 1310720 | tf_op jit(solution)/shard_map/all_gather | solution.py:51
  150.0 84.6 %all-to-all-start.1 = ((f32[4,112,3584]{2,1,0:T(8,128)}), f32[4,112,3584]{2,1,0:T(8,128)}, u32[]{:S(2)}, u32[]{:S(2)}) async-start(f32[4,112,3584]{2,1,0:T(8,128)} %bitcast.23), calls=%async_computation.1 | async-start | bytes 12845056 | tf_op jit(solution)/shard_map/all_to_all | solution.py:58
Sparse Core Ops, SparseCore 0:
  21.1 93.5 all-gather.3
  116.5 22.3 all-gather.5
where the time goes:
time: 276 us
  waiting for transfers between devices  116 us (42%)
  blocking collectives  90 us (33%)
  local copies, waits for them, and re-layouts  34.2 us (12%)
  between operations  14.2 us (5%)
  matrix products  8.66 us (3%)
  other arithmetic  7.27 us (3%)
  starting transfers between devices  5.32 us (2%)
    all_gather x1, waiting for transfers between devices, shards(): cols = lax.all_gather(own, PLANE, axis=0, tiled=True)  93.6 us
    psum x4, blocking collectives, shards(): total = lax.psum(total, axis)  78 us
    all_gather x1, waiting for transfers between devices, shards(): left = lax.all_gather(left, RING, axis=0)  22.4 us
    transpose x1, local copies, waits for them, and re-layouts, shards(): out = out.reshape(ring, rows // ring, tiles, LANES).transpose(1, 2, 0, 3)  12.1 us
    all_to_all x1, blocking collectives, shards(): lax.all_to_all(slots, (RING, 'exp'), split_axis=0, concat_axis=0, tiled=T...  11.9 us
    dot_general x1, matrix products, shards(): lax.dot_general(left, cols, (((0,), (0,)), ((), ())), preferred_element_t...  8.46 us
    reshape x1, local copies, waits for them, and re-layouts, shards(): return out.reshape(1, rows // ring, ff)  8.18 us
    reshape x1, local copies, waits for them, and re-layouts, shards(): out = out.reshape(ring, rows // ring, tiles, LANES).transpose(1, 2, 0, 3)  7.9 us
  transfers between devices with their start and end apart: 3, of which 2 were waited for; matrix products, arithmetic and copies ran while one was open for 0% of the time, Pallas kernels for 0%

commit v1 on v0

--- a/solution.py
+++ b/solution.py
@@ -41,7 +41,9 @@
     for axis in TOK_EXP:
         total = lax.psum(total, axis)
     routed_total = total[lax.axis_index("exp")]
-    cols = lax.all_gather(own, PLANE, axis=0, tiled=True)
+    cols = jnp.concatenate(
+        lax.all_to_all(jnp.stack([own] * lax.axis_size(PLANE)), PLANE, 0, 0), axis=0
+    )
     group = lax.axis_index("tok_0") * lax.axis_size("tok_1") + lax.axis_index("tok_1")
     rows = ff // lax.axis_size(PLANE)
     first = group * rows // LANES

time: 276 us -> 361 us (1.31)
  waiting for transfers between devices: 116 us -> 186 us
  starting transfers between devices: 5.32 us -> 16.5 us
    all_to_all x0 -> x1, waiting for transfers between devices: none -> 162 us  [shards(): lax.all_to_all(jnp.stack([own] * lax.axis_size(PLANE)), PLANE, 0, 0)]
    all_gather x1 -> x0, waiting for transfers between devices: 93.6 us -> none  [shards(): cols = lax.all_gather(own, PLANE, axis=0, tiled=True)]
    all_to_all x0 -> x1, starting transfers between devices: none -> 11.1 us  [shards(): lax.all_to_all(jnp.stack([own] * lax.axis_size(PLANE)), PLANE, 0, 0)]
    another operation x0 -> x2, local copies, waits for them, and re-layouts: none -> 3.91 us  [shards(): jnp.stack([own] * lax.axis_size(PLANE))]
where the time goes in v1:
time: 361 us; the launch traced here: 360 us
  waiting for transfers between devices  186 us (52%)
  blocking collectives  90 us (25%)
  local copies, waits for them, and re-layouts  37.4 us (10%)
  starting transfers between devices  16.5 us (5%)
  between operations  14.2 us (4%)
  matrix products  8.66 us (2%)
  other arithmetic  7.27 us (2%)
    all_to_all x1, waiting for transfers between devices, shards(): lax.all_to_all(jnp.stack([own] * lax.axis_size(PLANE)), PLANE, 0, 0)  162 us
    psum x4, blocking collectives, shards(): total = lax.psum(total, axis)  78 us
    all_gather x1, waiting for transfers between devices, shards(): left = lax.all_gather(left, RING, axis=0)  23.8 us
    transpose x1, local copies, waits for them, and re-layouts, shards(): out = out.reshape(ring, rows // ring, tiles, LANES).transpose(1, 2, 0, 3)  12.1 us
    all_to_all x1, blocking collectives, shards(): lax.all_to_all(slots, (RING, 'exp'), split_axis=0, concat_axis=0, tiled=T...  11.9 us
    all_to_all x1, starting transfers between devices, shards(): lax.all_to_all(jnp.stack([own] * lax.axis_size(PLANE)), PLANE, 0, 0)  11.1 us
    dot_general x1, matrix products, shards(): lax.dot_general(left, cols, (((0,), (0,)), ((), ())), preferred_element_t...  8.46 us
    reshape x1, local copies, waits for them, and re-layouts, shards(): return out.reshape(1, rows // ring, ff)  8.18 us
  transfers between devices with their start and end apart: 3, of which 2 were waited for; matrix products, arithmetic and copies ran while one was open for 0% of the time, Pallas kernels for 0%

profile of v1, /device:TPU:1, one launch (start us, length us, event | category | flops | bytes accessed | tf_op | source)
XLA Modules:
  0.0 360.2 jit_solution(1122569689451866635)
XLA Ops:
  6.5 0.7 compare_reduce_fusion
  7.3 0.2 reduce_window_sum.11
  7.5 0.1 copy-done
  7.6 0.2 convolution_convert_fusion
  7.8 0.1 reshape.82
  8.0 0.1 reshape.83
  8.1 0.1 copy.18
  8.3 11.9 %all_to_all.15 = bf16[8,4,3584]{2,1,0:T(4,128)(2,1)S(1)} all-to-all(bf16[8,4,3584]{2,1,0:T(4,128)(2,1)S(1)} %copy.18), channel_id=1, replica_groups=mesh['tok_0'=4,'tok_1'=8,'tok_2'=4,'exp'=2] {'tok_2','exp'}, dimensions={0} | all-to-all | bytes 458752 | tf_op jit(solution)/shard_map/all_to_all | solution.py:38
  20.2 0.1 stack_reshape.2
  20.2 3.9 %stack.3 = bf16[32,32,3584]{2,1,0:T(8,128)(2,1)} broadcast(bf16[32,3584]{1,0:T(8,128)(2,1)S(1)} %stack_reshape.2), dimensions={1,2} | broadcast | bytes 7569408 | tf_op jit(solution)/shard_map/stack | solution.py:45
  24.1 11.1 %all-to-all-start.1 = ((bf16[32,32,3584]{2,1,0:T(8,128)(2,1)}), bf16[32,32,3584]{2,1,0:T(8,128)(2,1)}, u32[]{:S(2)}, u32[]{:S(2)}) async-start(bf16[32,32,3584]{2,1,0:T(8,128)(2,1)} %stack.3), calls=%async_computation.1 | async-start | bytes 14680064 | tf_op jit(solution)/shard_map/all_to_all | solution.py:45
  35.3 0.0 all-gather.3.cloned.1.call-start
  35.4 162.5 %all-to-all-done.1 = bf16[32,32,3584]{2,1,0:T(8,128)(2,1)} async-done(((bf16[32,32,3584]{2,1,0:T(8,128)(2,1)}), bf16[32,32,3584]{2,1,0:T(8,128)(2,1)}, u32[]{:S(2)}, u32[]{:S(2)}) %all-to-all-start.1) | async-done | bytes 7340064 | tf_op jit(solution)/shard_map/all_to_all | solution.py:45
  197.8 1.7 constant_dynamic-slice_fusion.1
  199.5 0.0 all-gather.3.cloned.1.call-update
  199.6 23.8 %all-gather.3.cloned.1.call-done = bf16[4096,128]{1,0:T(8,128)(2,1)} async-done(((bf16[1024,128]{1,0:T(8,128)(2,1)}), bf16[4096,128]{1,0:T(8,128)(2,1)}) %all-gather.3.cloned.1.call-update) | async-done | bytes 1048592 | tf_op jit(solution)/shard_map/all_gather | solution.py:53
  223.3 2.0 gather_fusion
  225.3 0.2 select_bitcast_fusion
  225.5 0.5 copy.19
  226.0 0.1 constant_dynamic-slice_fusion
  226.1 8.5 %fusion.8 = f32[4,112,3584]{2,1,0:T(8,128)} fusion(bf16[4,112,1024]{2,1,0:T(8,128)(2,1)S(1)} %bitcast.32, bf16[1024,3584,1]{1,0,2:T(8,128)(2,1)} %bitcast.11), kind=kOutput, calls=%fused_computation.29 | convolution fusion | flops 3288334336 | bytes 14680064 | tf_op jit(solution)/shard_map/dot_general | solution.py:57
  234.6 5.3 %all-to-all-start.2 = ((f32[4,112,3584]{2,1,0:T(8,128)}), f32[4,112,3584]{2,1,0:T(8,128)}, u32[]{:S(2)}, u32[]{:S(2)}) async-start(f32[4,112,3584]{2,1,0:T(8,128)} %fusion.8), calls=%async_computation.2 | async-start | bytes 12845056 | tf_op jit(solution)/shard_map/all_to_all | solution.py:60
  239.8 0.1 convert_reduce_fusion
  240.0 8.8 %psum.28 = f32[2]{0:T(128)S(1)} all-reduce(f32[2]{0:T(128)S(1)} %convert_element_type.14), channel_id=1, replica_groups=mesh['tok_0'=4,'tok_1'=8,'tok_2'=4,'exp'=2] {'tok_0'}, use_global_device_ids=true, to_apply=%region_3.4 | all-reduce | flops 2 | bytes 16 | tf_op jit(solution)/shard_map/psum | solution.py:42
  248.8 15.3 %psum.29 = f32[2]{0:T(128)S(1)} all-reduce(f32[2]{0:T(128)S(1)} %psum.28), channel_id=1, replica_groups=mesh['tok_0'=4,'tok_1'=8,'tok_2'=4,'exp'=2] {'tok_1'}, use_global_device_ids=true, to_apply=%region_4.5 | all-reduce | flops 2 | bytes 16 | tf_op jit(solution)/shard_map/psum | solution.py:42
  264.1 48.1 %psum.30 = f32[2]{0:T(128)S(1)} all-reduce(f32[2]{0:T(128)S(1)} %psum.29), channel_id=1, replica_groups=mesh['tok_0'=4,'tok_1'=8,'tok_2'=4,'exp'=2] {'tok_2'}, use_global_device_ids=true, to_apply=%region_5.6 | all-reduce | flops 2 | bytes 16 | tf_op jit(solution)/shard_map/psum | solution.py:42
  312.1 5.9 %psum.31 = f32[2]{0:T(128)S(1)} all-reduce(f32[2]{0:T(128)S(1)} %psum.30), channel_id=1, replica_groups=mesh['tok_0'=4,'tok_1'=8,'tok_2'=4,'exp'=2] {'exp'}, use_global_device_ids=true, to_apply=%region_6.7 | all-reduce | flops 2 | bytes 16 | tf_op jit(solution)/shard_map/psum | solution.py:42
  318.0 0.6 dynamic_slice.11
  319.2 6.0 %broadcast_multiply_fusion = f32[4,112,3584]{2,1,0:T(8,128)} fusion(f32[4,112,3584]{2,1,0:T(8,128)} %all-to-all-done.2, f32[]{:T(128)} %bitcast.12), kind=kLoop, calls=%fused_computation.2 | loop fusion | flops 1605632 | bytes 12845060 | tf_op jit(solution)/shard_map/mul | solution.py:67
  325.2 7.9 %reshape.86 = f32[4,112,28,128]{3,2,1,0:T(8,128)} reshape(f32[4,112,3584]{2,1,0:T(8,128)} %broadcast_multiply_fusion) | data formatting | bytes 12845056 | tf_op jit(solution)/shard_map/reshape | solution.py:68
  333.1 12.1 %copy.20 = f32[112,28,4,128]{3,2,1,0:T(4,128)} copy(f32[112,28,4,128]{3,1,0,2:T(8,128)} %bitcast.28) | data formatting | bytes 12845056 | tf_op jit(solution)/shard_map/transpose | solution.py:68
  345.2 8.2 %reshape.87 = f32[1,112,14336]{2,1,0:T(8,128)} reshape(f32[112,28,4,128]{3,2,1,0:T(4,128)} %copy.20) | data formatting | bytes 12845056 | tf_op jit(solution)/shard_map/reshape | solution.py:69
  (9 shorter events, 0.1 us)
Async XLA Ops:
  6.5 1.0 copy-start
  24.1 173.7 %all-to-all-start.1 = ((bf16[32,32,3584]{2,1,0:T(8,128)(2,1)}), bf16[32,32,3584]{2,1,0:T(8,128)(2,1)}, u32[]{:S(2)}, u32[]{:S(2)}) async-start(bf16[32,32,3584]{2,1,0:T(8,128)(2,1)} %stack.3), calls=%async_computation.1 | async-start | bytes 14680064 | tf_op jit(solution)/shard_map/all_to_all | solution.py:45
  35.3 188.1 %all-gather.3.cloned.1.call-start = ((), (), s32[]{:S(2)}) async-start(), calls=%async_computation.3 | async-start | bytes 1310720 | tf_op jit(solution)/shard_map/all_gather | solution.py:53
  234.6 84.6 %all-to-all-start.2 = ((f32[4,112,3584]{2,1,0:T(8,128)}), f32[4,112,3584]{2,1,0:T(8,128)}, u32[]{:S(2)}, u32[]{:S(2)}) async-start(f32[4,112,3584]{2,1,0:T(8,128)} %fusion.8), calls=%async_computation.2 | async-start | bytes 12845056 | tf_op jit(solution)/shard_map/all_to_all | solution.py:60
Sparse Core Ops, SparseCore 0:
  199.7 23.6 all-gather.2
